TPU v7x, 32 devices: a whole 2x2x4 slice. The times are simulated.
32 devices in a mesh: node: 8 (over z, y), local: 4 (over x, core).
Axes of the slice: x: 2, y: 2, z: 4, core: 2. Of those that a mesh axis runs over, the one named last changes fastest.
Arguments:
- tokens: bfloat16 [4096, 2048], P(('node', 'local')), may hold values from -6 to 6
- norm_gain: float32 [2048], replicated, may hold values from 0.1 to 1.9
- router_weight: bfloat16 [2048, 16], replicated, may hold values from -0.125 to 0.125
- placement: int32 [16], replicated, may hold values from 0 to 15, each once
- expert_ids: int32 [4096, 6], P(('node', 'local')), may hold values from 0 to 15, all different within a row; in each aligned block of 128 rows (0 to 127, 128 to 255, ...) at most 72 rows name the same one
- w_gate: bfloat16 [2048, 22528], P(None, ('node', 'local')), may hold values from -0.125 to 0.125
- w_up: bfloat16 [2048, 22528], P(None, ('node', 'local')), may hold values from -0.125 to 0.125
- w_down: bfloat16 [22528, 2048], P(('node', 'local')), may hold values from -0.15625 to 0.15625
- shared_gate: bfloat16 [2048, 2816], P(None, 'local'), may hold values from -0.125 to 0.125
- shared_up: bfloat16 [2048, 2816], P(None, 'local'), may hold values from -0.125 to 0.125
- shared_down: bfloat16 [2816, 2048], P('local'), may hold values from -0.109375 to 0.109375
Outputs:
- moe_out: bfloat16 [4096, 2048], P(('node', 'local'))
Inputs may be any that keep to these rules, and one draw needn't show every extreme that they name: Expert e's weights stand in slot placement[e]; every slot holds one expert. `expert_ids`: each row names 6 different experts. Among the rows of one device (aligned blocks of 128 rows) no expert is named more than 72 times, a bound that some block reaches.
All inputs are finite; a program needn't handle non-finite values.
Results may differ from a plain program's by a relative error of at most 0.011.
Values may be sent and summed in bfloat16 or wider, within the bound.
A program may use at most 128 MiB of HBM per device.

v0:
```python
import jax
import jax.numpy as jnp
from jax import lax
from jax.sharding import PartitionSpec as P


def partner_2(block, axis, bit):
    count = lax.axis_size(axis)
    route = []
    for low in range(count):
        high = low | 1 << bit
        if high != low and high < count:
            route += [(low, high), (high, low)]
    return lax.ppermute(block, axis, route)


def feed_forward(row_block, gate_cols, up_cols, down_rows):
    gate_proj = jnp.dot(row_block, gate_cols, preferred_element_type=jnp.float32)
    up_proj = jnp.dot(row_block, up_cols, preferred_element_type=jnp.float32)
    activated = (jax.nn.silu(gate_proj) * up_proj).astype(jnp.bfloat16)
    return jnp.dot(activated, down_rows, preferred_element_type=jnp.float32)


def body(
    tokens,
    norm_gain,
    router_weight,
    placement,
    expert_ids,
    w_gate,
    w_up,
    w_down,
    shared_gate,
    shared_up,
    shared_down,
):
    floats = tokens.astype(jnp.float32)
    normed = (
        floats * lax.rsqrt(jnp.mean(floats * floats, -1, keepdims=True) + 1e-06) * norm_gain
    ).astype(jnp.bfloat16)
    tok_rows = normed.shape[0]
    model_width = normed.shape[1]
    gathered = lax.all_gather(normed, "local", axis=0, tiled=True)
    shared = lax.psum_scatter(
        feed_forward(gathered, shared_gate, shared_up, shared_down),
        "local",
        scatter_dimension=0,
        tiled=True,
    )
    top_count = expert_ids.shape[1]
    experts = placement.shape[0]
    capacity = 3 * tok_rows * top_count // (2 * experts)
    logits = jnp.dot(normed, router_weight, preferred_element_type=jnp.float32)
    scores = jax.nn.sigmoid(logits)
    expert_iota = jnp.arange(experts, dtype=jnp.int32)
    id_hot = expert_ids[:, :, None] == expert_iota
    picked = jnp.sum(jnp.where(id_hot, scores[:, None, :], 0.0), -1)
    gate_weights = (picked / jnp.sum(picked, -1, keepdims=True)).astype(jnp.bfloat16)
    slots = jnp.sum(jnp.where(id_hot, placement[None, None, :], 0), -1)
    slot_hot = (
        (slots[:, :, None] == expert_iota).reshape(tok_rows * top_count, experts).astype(jnp.int32)
    )
    running = jnp.cumsum(slot_hot, 0) - 1
    position = jnp.sum(running * slot_hot, -1)
    column = slots.reshape(-1) * capacity + position
    column_iota = jnp.arange(experts * capacity, dtype=jnp.int32)
    place_hot = (column[:, None] == column_iota).reshape(tok_rows, top_count, experts * capacity)
    dispatch = jnp.any(place_hot, 1).astype(jnp.bfloat16)
    combine = jnp.sum(
        jnp.where(place_hot, gate_weights[:, :, None].astype(jnp.float32), 0.0), 1
    ).astype(jnp.bfloat16)
    flat_rows = lax.dot_general(
        dispatch, normed, (((0,), (0,)), ((), ())), preferred_element_type=jnp.float32
    ).astype(jnp.bfloat16)
    node_count = lax.axis_size("node")
    local_count = lax.axis_size("local")
    peer_count = node_count * local_count
    outgoing = flat_rows.reshape(peer_count, capacity // 2, model_width)
    piece = lax.all_to_all(outgoing, ("node", "local"), split_axis=0, concat_axis=0, tiled=True)
    partner = partner_2(piece, "local", 0)
    joined = jnp.concatenate([piece, partner], 1)
    result = feed_forward(joined.reshape(-1, model_width), w_gate, w_up, w_down).astype(
        jnp.bfloat16
    )
    result = result.reshape(joined.shape)
    own_part = result[:, : piece.shape[1]]
    their_part = result[:, piece.shape[1] :]
    back_part = partner_2(their_part, "local", 0)
    answers = (own_part.astype(jnp.float32) + back_part.astype(jnp.float32)).astype(jnp.bfloat16)
    returned = lax.all_to_all(answers, ("node", "local"), split_axis=0, concat_axis=0, tiled=True)
    expert_out = returned.reshape(experts * capacity, model_width)
    routed = jnp.dot(combine, expert_out, preferred_element_type=jnp.float32)
    return (shared + routed).astype(jnp.bfloat16)


def solution(mesh):
    in_specs = (
        P(("node", "local"), None),
        P(),
        P(),
        P(),
        P(("node", "local"), None),
        P(None, ("node", "local")),
        P(None, ("node", "local")),
        P(("node", "local"), None),
        P(None, "local"),
        P(None, "local"),
        P("local", None),
    )
    out_specs = P(("node", "local"), None)
    return jax.shard_map(body, mesh=mesh, in_specs=in_specs, out_specs=out_specs, check_vma=False)
```

profile of v0, /device:TPU:0, one launch (start us, length us, event | category | flops | bytes accessed | tf_op | source)
XLA Modules:
  0.0 398.6 jit_solution(89104451697808257)
XLA Ops:
  6.5 0.0 copy-start
  6.5 0.0 all-gather.2.cloned.1.call-start
  6.5 0.9 select_reduce_fusion.3
  7.5 0.1 copy.33
  7.6 0.1 eq.60
  7.7 0.1 eq.56
  7.9 1.7 reduce-window.6
  9.6 0.3 slice_reduce_fusion
  9.9 0.1 fusion.13
  10.0 0.1 reduce_sum.59
  10.1 0.1 copy.36
  10.2 0.6 fusion
  10.8 1.2 fusion.7
  12.0 1.2 fusion.9
  13.3 0.0 copy-start.3
  13.3 3.6 convolution_convert_fusion.1
  16.9 7.2 %reshape.84 = bf16[32,36,2048]{2,1,0:T(8,128)(2,1)} reshape(bf16[1152,2048]{1,0:T(8,128)(2,1)} %convolution_convert_fusion.1) | data formatting | bytes 9437184 | tf_op jit(solution)/shard_map/reshape | solution.py:78
  24.1 123.6 %all_to_all.10 = bf16[32,36,2048]{2,1,0:T(8,128)(2,1)S(1)} all-to-all(bf16[32,36,2048]{2,1,0:T(8,128)(2,1)} %reshape.84), channel_id=1, replica_groups=mesh['node'=8,'local'=4] {'node','local'}, dimensions={0} | all-to-all | bytes 9437184 | tf_op jit(solution)/shard_map/all_to_all | solution.py:79
  147.7 2.6 copy.37
  150.3 0.1 collective-permute-start
  150.4 7.9 %collective-permute-done = bf16[32,36,2048]{2,0,1:T(8,128)(2,1)S(1)} collective-permute-done((bf16[32,36,2048]{2,0,1:T(8,128)(2,1)S(1)}, bf16[32,36,2048]{2,0,1:T(8,128)(2,1)S(1)}, u32[]{:S(2)}, u32[]{:S(2)}) %collective-permute-start) | collective-permute-done | bytes 4718624 | tf_op jit(solution)/shard_map/ppermute | solution.py:14
  158.2 2.6 copy.38
  160.9 0.0 copy-start.9
  160.9 2.4 pad_maximum_fusion
  163.3 3.6 copy-done.2
  167.0 9.0 %fusion.20 = f32[2304,704]{0,1:T(8,128)} fusion(bf16[2304,2048]{1,0:T(8,128)(2,1)S(1)} %bitcast.35, bf16[2048,704]{0,1:T(8,128)(2,1)S(1)} %copy-done.9), kind=kOutput, calls=%fused_computation.44 | convolution fusion | flops 6643777536 | bytes 18808832 | tf_op jit(solution)/shard_map/dot_general | solution.py:18
  175.9 24.9 %convolution_convert_fusion = bf16[2304,2048]{1,0:T(8,128)(2,1)} fusion(bf16[704,2048]{1,0:T(8,128)(2,1)S(1)} %copy-done, f32[2304,704]{0,1:T(8,128)} %fusion.20, bf16[2304,2048]{1,0:T(8,128)(2,1)} %bitcast.36, bf16[2048,704]{0,1:T(8,128)(2,1)} %param.17), kind=kOutput, calls=%fused_computation | convolution fusion | flops 13302005760 | bytes 31129600 | tf_op jit(solution)/shard_map/dot_general | solution.py:21
  200.8 11.5 %fusion.18 = (bf16[32,36,2048]{2,1,0:T(8,128)(2,1)}, bf16[32,36,2048]{2,1,0:T(8,128)(2,1)}) fusion(bf16[32,72,2048]{2,1,0:T(8,128)(2,1)} %bitcast.34), kind=kLoop, calls=%fused_computation.42 | loop fusion | bytes 18874368 | tf_op jit(solution)/shard_map/slice | solution.py:86
  212.4 7.3 %copy.43 = bf16[32,36,2048]{2,0,1:T(8,128)(2,1)} copy(bf16[32,36,2048]{2,1,0:T(8,128)(2,1)} %get-tuple-element.8) | data formatting | bytes 9437184
  219.7 0.1 collective-permute-start.1
  219.8 0.0 all-gather.2.cloned.1.call-update
  219.9 21.9 %all-gather.2.cloned.1.call-done = bf16[512,2048]{1,0:T(8,128)(2,1)} async-done(((bf16[128,2048]{1,0:T(8,128)(2,1)}), bf16[512,2048]{1,0:T(8,128)(2,1)}) %all-gather.2.cloned.1.call-update) | async-done | bytes 2097168 | tf_op jit(solution)/shard_map/all_gather | solution.py:43
  241.7 4.4 %fusion.19 = f32[512,704]{0,1:T(8,128)} fusion(bf16[512,2048]{1,0:T(8,128)(2,1)} %all-gather.2.cloned.1.call-done, bf16[2048,704]{0,1:T(8,128)(2,1)S(1)} %copy-done.10), kind=kOutput, calls=%fused_computation.43 | convolution fusion | flops 1476395008 | bytes 6422528 | tf_op jit(solution)/shard_map/dot_general | solution.py:18
  246.1 0.0 collective-permute-done.1
  246.1 7.1 %add_convert_fusion = bf16[32,36,2048]{2,0,1:T(8,128)(2,1)S(1)} fusion(bf16[32,36,2048]{2,0,1:T(8,128)(2,1)} %collective-permute-done.1, bf16[32,36,2048]{2,1,0:T(8,128)(2,1)} %get-tuple-element.7), kind=kLoop, calls=%fused_computation.2 | loop fusion | flops 9437184 | bytes 14155776 | tf_op jit(solution)/shard_map/convert_element_type | solution.py:89
  253.2 5.2 %copy.41 = bf16[32,36,2048]{2,1,0:T(8,128)(2,1)} copy(bf16[32,36,2048]{2,0,1:T(8,128)(2,1)S(1)} %add_convert_fusion) | data formatting | bytes 9437184 | tf_op jit(solution)/shard_map/convert_element_type | solution.py:89
  258.4 4.7 %all-to-all-start.1 = ((bf16[32,36,2048]{2,1,0:T(8,128)(2,1)}), bf16[32,36,2048]{2,1,0:T(8,128)(2,1)}, u32[]{:S(2)}, u32[]{:S(2)}) async-start(bf16[32,36,2048]{2,1,0:T(8,128)(2,1)} %copy.41), calls=%async_computation.2 | async-start | bytes 10485760 | tf_op jit(solution)/shard_map/all_to_all | solution.py:90
  263.2 0.0 copy-start.4
  263.2 0.0 copy-start.5
  263.2 0.0 reduce-scatter.2.cloned.1.call-start
  263.2 8.7 %fusion.10 = f32[512,2048]{1,0:T(8,128)} fusion(bf16[704,2048]{1,0:T(8,128)(2,1)} %param.21, bf16[512,2048]{1,0:T(8,128)(2,1)S(1)} %copy-done.11, bf16[2048,704]{0,1:T(8,128)(2,1)} %param.20, f32[512,704]{0,1:T(8,128)} %fusion.19), kind=kOutput, calls=%fused_computation.22 | convolution fusion | flops 2954952704 | bytes 13500416 | tf_op jit(solution)/shard_map/dot_general | solution.py:21
  271.9 0.0 reduce-scatter.2.cloned.1.call-update
  272.0 0.2 fusion.6
  272.2 0.4 copy-done.8
  272.7 0.5 select_reduce_fusion
  273.2 106.5 %all-to-all-done.1 = bf16[32,36,2048]{2,1,0:T(8,128)(2,1)} async-done(((bf16[32,36,2048]{2,1,0:T(8,128)(2,1)}), bf16[32,36,2048]{2,1,0:T(8,128)(2,1)}, u32[]{:S(2)}, u32[]{:S(2)}) %all-to-all-start.1) | async-done | bytes 4718624 | tf_op jit(solution)/shard_map/all_to_all | solution.py:90
  379.7 7.4 %reshape.87 = bf16[1152,2048]{1,0:T(8,128)(2,1)} reshape(bf16[32,36,2048]{2,1,0:T(8,128)(2,1)} %all-to-all-done.1) | data formatting | bytes 9437184 | tf_op jit(solution)/shard_map/reshape | solution.py:91
  387.1 4.3 %fusion.2 = bf16[128,2048]{1,0:T(8,128)(2,1)} fusion(f32[128,2048]{1,0:T(8,128)} %reduce-scatter.2.cloned.1.call-done, bf16[1152,2048]{1,0:T(8,128)(2,1)} %reshape.87, bf16[128,1152]{1,0:T(8,128)(2,1)S(1)} %select_reduce_fusion), kind=kOutput, calls=%fused_computation.10 | convolution fusion | flops 604504064 | bytes 6586368 | tf_op jit(solution)/shard_map/dot_general | solution.py:92
  (24 shorter events, 0.1 us)
Async XLA Ops:
  6.5 169.4 %copy-start = (bf16[704,2048]{1,0:T(8,128)(2,1)S(1)}, bf16[704,2048]{1,0:T(8,128)(2,1)}, u32[]{:S(2)}) copy-start(bf16[704,2048]{1,0:T(8,128)(2,1)} %param.18) | copy-start | bytes 8650756
  6.5 235.2 %all-gather.2.cloned.1.call-start = ((), (), s32[]{:S(2)}) async-start(), calls=%async_computation.3 | async-start | bytes 2621440 | tf_op jit(solution)/shard_map/all_gather | solution.py:43
  10.2 1.8 copy-start.6
  13.3 10.8 %copy-start.3 = (bf16[128,2048]{1,0:T(8,128)(2,1)}, bf16[128,2048]{1,0:T(8,128)(2,1)S(1)}, u32[]{:S(2)}) copy-start(bf16[128,2048]{1,0:T(8,128)(2,1)S(1)} %fusion.9) | copy-start | bytes 1572868
  150.3 8.0 %collective-permute-start = (bf16[32,36,2048]{2,0,1:T(8,128)(2,1)S(1)}, bf16[32,36,2048]{2,0,1:T(8,128)(2,1)S(1)}, u32[]{:S(2)}, u32[]{:S(2)}) collective-permute-start(bf16[32,36,2048]{2,0,1:T(8,128)(2,1)S(1)} %copy.37), channel_id=1, source_target_pairs={{0,1},{1,0},{2,3},{3,2},{4,5},{5,4},{6,7},{7,6},{8,9},{9,8},{10,11... | collective-permute-start | bytes 14155784 | tf_op jit(solution)/shard_map/ppermute | solution.py:14
  160.9 6.1 %copy-start.9 = (bf16[2048,704]{0,1:T(8,128)(2,1)S(1)}, bf16[2048,704]{0,1:T(8,128)(2,1)}, u32[]{:S(2)}) copy-start(bf16[2048,704]{0,1:T(8,128)(2,1)} %param.16) | copy-start | bytes 8650756
  163.3 3.7 copy-start.2
  212.3 29.4 %copy-start.10 = (bf16[2048,704]{0,1:T(8,128)(2,1)S(1)}, bf16[2048,704]{0,1:T(8,128)(2,1)}, u32[]{:S(2)}) copy-start(bf16[2048,704]{0,1:T(8,128)(2,1)} %param.19) | copy-start | bytes 8650756
  219.7 26.4 %collective-permute-start.1 = (bf16[32,36,2048]{2,0,1:T(8,128)(2,1)}, bf16[32,36,2048]{2,0,1:T(8,128)(2,1)}, u32[]{:S(2)}, u32[]{:S(2)}) collective-permute-start(bf16[32,36,2048]{2,0,1:T(8,128)(2,1)} %copy.43), channel_id=1, source_target_pairs={{0,1},{1,0},{2,3},{3,2},{4,5},{5,4},{6,7},{7,6},{8,9},{9,8},{10,11... | collective-permute-start | bytes 14155784 | tf_op jit(solution)/shard_map/ppermute | solution.py:14
  258.4 4.8 %copy-start.11 = (bf16[512,2048]{1,0:T(8,128)(2,1)S(1)}, bf16[512,2048]{1,0:T(8,128)(2,1)}, u32[]{:S(2)}) copy-start(bf16[512,2048]{1,0:T(8,128)(2,1)} %all-gather.2.cloned.1.call-done) | copy-start | bytes 6291460
  258.4 121.3 %all-to-all-start.1 = ((bf16[32,36,2048]{2,1,0:T(8,128)(2,1)}), bf16[32,36,2048]{2,1,0:T(8,128)(2,1)}, u32[]{:S(2)}, u32[]{:S(2)}) async-start(bf16[32,36,2048]{2,1,0:T(8,128)(2,1)} %copy.41), calls=%async_computation.2 | async-start | bytes 10485760 | tf_op jit(solution)/shard_map/all_to_all | solution.py:90
  263.2 8.8 %copy-start.4 = (bf16[128,2048]{1,0:T(8,128)(2,1)S(1)}, bf16[128,2048]{1,0:T(8,128)(2,1)}, u32[]{:S(2)}) copy-start(bf16[128,2048]{1,0:T(8,128)(2,1)} %copy-done.3) | copy-start | bytes 1572868
  263.2 8.8 %copy-start.5 = (bf16[2048,16]{0,1:T(8,128)(2,1)S(1)}, bf16[2048,16]{0,1:T(8,128)(2,1)}, u32[]{:S(2)}) copy-start(bf16[2048,16]{0,1:T(8,128)(2,1)} %param.13) | copy-start | bytes 196612
  263.2 123.9 %reduce-scatter.2.cloned.1.call-start = ((), (), s32[]{:S(2)}) async-start(), calls=%async_computation.4 | async-start | bytes 5242880 | tf_op jit(solution)/shard_map/reduce_scatter | solution.py:44
  271.9 0.7 copy-start.8
  271.9 0.7 copy-start.7
  379.7 11.7 %copy-start.1 = (bf16[704,2048]{1,0:T(8,128)(2,1)S(1)}, bf16[704,2048]{1,0:T(8,128)(2,1)}, u32[]{:S(2)}) copy-start(bf16[704,2048]{1,0:T(8,128)(2,1)} %param.18) | copy-start | bytes 8650756
Sparse Core Ops, SparseCore 0:
  220.0 21.6 all-gather.1
  272.1 68.0 reduce-scatter.1
where the time goes:
time: 402 us; the launch traced here: 399 us
  waiting for transfers between devices  136 us (34%)
  blocking collectives  124 us (31%)
  matrix products  55.1 us (14%)
  local copies, waits for them, and re-layouts  48.8 us (12%)
  other arithmetic  15.9 us (4%)
  between operations  14 us (3%)
  starting transfers between devices  4.97 us (1%)
    all_to_all x1, blocking collectives, body(): lax.all_to_all(outgoing, ('node', 'local'), split_axis=0, concat_axis=0,...  124 us
    all_to_all x1, waiting for transfers between devices, body(): lax.all_to_all(answers, ('node', 'local'), split_axis=0, concat_axis=0, t...  107 us
    dot_general x2, matrix products, feed_forward(): return jnp.dot(activated, down_rows, preferred_element_type=jnp.float32)  33.6 us
    all_gather x1, waiting for transfers between devices, body(): gathered = lax.all_gather(normed, 'local', axis=0, tiled=True)  21.9 us
    dot_general x2, matrix products, feed_forward(): jnp.dot(row_block, gate_cols, preferred_element_type=jnp.float32)  13.4 us
    slice x1, local copies, waits for them, and re-layouts, body(): own_part = result[:, :piece.shape[1]]  11.5 us
    unnamed x25, local copies, waits for them, and re-layouts  11.4 us
  transfers between devices with their start and end apart: 5, of which 3 were waited for; matrix products, arithmetic and copies ran while one was open for 5% of the time, Pallas kernels for 0%

commit v1 on v0

--- a/solution.py
+++ b/solution.py
@@ -1,6 +1,8 @@
 import jax
 import jax.numpy as jnp
 from jax import lax
+from jax.experimental import pallas as pl
+from jax.experimental.pallas import tpu as pltpu
 from jax.sharding import PartitionSpec as P
 
 
@@ -93,6 +95,382 @@
     return (shared + routed).astype(jnp.bfloat16)
 
 
+MESH = pl.DeviceIdType.MESH
+
+
+class Place:
+    def __init__(self, depth):
+        node, local = lax.axis_index("node"), lax.axis_index("local")
+        self.depth = depth
+        self.z, self.y = node // 2, node % 2
+        self.x, self.c = local // 2, local % 2
+
+    def device(self, z, y, x, c):
+        return (z * 2 + y, x * 2 + c)
+
+    def block(self, z, y, x, c):
+        return ((z * 2 + y) * 2 + x) * 2 + c
+
+    def spot(self, p):
+        x = 1 - self.x if p & 1 else self.x
+        y = 1 - self.y if p & 2 else self.y
+        return y, x
+
+    def greet(self):
+        barrier = pltpu.get_barrier_semaphore()
+        z, y, x, c = self.z, self.y, self.x, self.c
+
+        def hello(z, y, x, c):
+            pl.semaphore_signal(
+                barrier, inc=1, device_id=self.device(z, y, x, c), device_id_type=MESH
+            )
+
+        hello(z, y, x, 1 - c)
+        hello(z, y, 1 - x, c)
+        hello(z, 1 - y, x, c)
+        pl.when(z > 0)(lambda: hello(z - 1, y, x, c))
+        pl.when(z < self.depth - 1)(lambda: hello(z + 1, y, x, c))
+        below = (z + self.depth - 1) // self.depth
+        above = (2 * self.depth - 2 - z) // self.depth
+        pl.semaphore_wait(barrier, 3 + below + above)
+
+    def at_distance(self, far, visit):
+        for off in (0,) if far == 0 else (-far, far):
+            other = self.z + off
+            ok = other >= 0 if off <= 0 else other < self.depth
+            pl.when(ok)(lambda off=off, other=other: visit(off, other))
+
+
+def remote(src, dst, send, recv, device):
+    return pltpu.make_async_remote_copy(
+        src_ref=src, dst_ref=dst, send_sem=send, recv_sem=recv, device_id=device, device_id_type=MESH
+    )
+
+
+def gather_kernel(
+    depth, rows, own, out, home_sem, zsend, zrecv, psend, precv, fsend, frecv, csend, crecv
+):
+    at = Place(depth)
+    z, y, x, c = at.z, at.y, at.x, at.c
+    half = rows // 2
+    at.greet()
+    xdev, ydev = at.device(z, y, 1 - x, c), at.device(z, 1 - y, x, c)
+    partner = at.device(z, y, x, 1 - c)
+
+    def whole(p, zz):
+        yy, xx = at.spot(p)
+        return out.at[at.block(zz, yy, xx, c)]
+
+    def part(p, zz, h):
+        return whole(p, zz).at[pl.ds(h * half, half)]
+
+    def zcopy(zz, up):
+        src = out.at[at.block(zz, y, x, c)]
+        way = 1 if up else 0
+        to = at.device(z + 1 if up else z - 1, y, x, c)
+        return remote(src, src, zsend.at[zz, way], zrecv.at[zz], to)
+
+    def plane(p, zz, h):
+        return remote(
+            part(0, zz, h), part(0, zz, h), psend.at[p - 1, zz, h], precv.at[p - 1, zz, h],
+            xdev if p == 1 else ydev,
+        )
+
+    def relay(p, zz):
+        h = p - 1
+        return remote(
+            part(p, zz, h), part(p, zz, h), fsend.at[h, zz], frecv.at[h, zz],
+            ydev if p == 1 else xdev,
+        )
+
+    def cross(p, zz):
+        return remote(whole(p, zz), whole(p, zz), csend.at[p, zz], crecv.at[p, zz], partner)
+
+    def first(off, zz):
+        if off == 0:
+            home = pltpu.make_async_copy(own, whole(0, zz), home_sem)
+            home.start()
+            home.wait()
+            pl.when(z > 0)(lambda: zcopy(zz, False).start())
+            pl.when(z < depth - 1)(lambda: zcopy(zz, True).start())
+        else:
+            zcopy(zz, True).wait_recv()
+            if off < 0:
+                pl.when(z < depth - 1)(lambda: zcopy(zz, True).start())
+            else:
+                pl.when(z > 0)(lambda: zcopy(zz, False).start())
+        plane(1, zz, 0).start()
+        plane(2, zz, 1).start()
+        plane(1, zz, 1).start()
+        plane(2, zz, 0).start()
+        cross(0, zz).start()
+
+    def second(off, zz):
+        plane(1, zz, 0).wait_recv()
+        relay(1, zz).start()
+        plane(2, zz, 1).wait_recv()
+        relay(2, zz).start()
+
+    def third(off, zz):
+        plane(1, zz, 1).wait_recv()
+        cross(1, zz).start()
+        plane(2, zz, 0).wait_recv()
+        cross(2, zz).start()
+        relay(1, zz).wait_recv()
+        relay(2, zz).wait_recv()
+        cross(3, zz).start()
+
+    def finish(off, zz):
+        if off <= 0:
+            pl.when(z < depth - 1)(lambda: zcopy(zz, True).wait_send())
+        if off >= 0:
+            pl.when(z > 0)(lambda: zcopy(zz, False).wait_send())
+        for p in (1, 2):
+            plane(p, zz, 0).wait_send()
+            plane(p, zz, 1).wait_send()
+            relay(p, zz).wait_send()
+        for p in range(4):
+            cross(p, zz).wait_send()
+            cross(p, zz).wait_recv()
+
+    work = []
+    for far in range(depth):
+        work += [(2 * far, 0, first, far), (2 * far + 1, 1, second, far), (2 * far + 4, 2, third, far)]
+    for _, _, visit, far in sorted(work, key=lambda w: w[:2]):
+        at.at_distance(far, visit)
+    for far in range(depth):
+        at.at_distance(far, finish)
+
+
+def gather_rows(own, depth, peers):
+    rows, width = own.shape
+    sem = pltpu.SemaphoreType.DMA
+    return pl.pallas_call(
+        lambda *refs: gather_kernel(depth, rows, *refs),
+        out_shape=jax.ShapeDtypeStruct((peers, rows, width), own.dtype),
+        in_specs=[pl.BlockSpec(memory_space=pltpu.VMEM)],
+        out_specs=pl.BlockSpec(memory_space=pl.ANY),
+        scratch_shapes=[
+            sem(()), sem((depth, 2)), sem((depth,)), sem((2, depth, 2)), sem((2, depth, 2)),
+            sem((2, depth)), sem((2, depth)), sem((4, depth)), sem((4, depth)),
+        ],
+        compiler_params=pltpu.CompilerParams(collective_id=0, has_side_effects=True),
+        name="gather_rows",
+    )(own)
+
+
+def scatter_kernel(
+    depth, rows, sums, out, mine, theirs, turned, plane_in, z_in,
+    load_sem, csend, crecv, fsend, frecv, psend, precv, zsend, zrecv,
+):
+    at = Place(depth)
+    z, y, x, c = at.z, at.y, at.x, at.c
+    half = rows // 2
+    step = 16
+    xdev, ydev = at.device(z, y, 1 - x, c), at.device(z, 1 - y, x, c)
+    partner = at.device(z, y, x, 1 - c)
+
+    def load(p, zz):
+        yy, xx = at.spot(p)
+        return pltpu.make_async_copy(
+            sums.at[at.block(zz, yy, xx, c)], mine.at[p, zz], load_sem.at[p, zz]
+        )
+
+    def cross(p, zz):
+        yy, xx = at.spot(p)
+        return remote(
+            sums.at[at.block(zz, yy, xx, 1 - c)], theirs.at[p, zz],
+            csend.at[p, zz], crecv.at[p, zz], partner,
+        )
+
+    def turn(p, zz):
+        h = p - 1
+        return remote(
+            mine.at[3, zz, pl.ds(h * half, half)], turned.at[h, zz],
+            fsend.at[h, zz], frecv.at[h, zz], xdev if p == 1 else ydev,
+        )
+
+    def plane(p, zz, h):
+        piece = pl.ds(h * half, half)
+        return remote(
+            mine.at[p, zz, piece], plane_in.at[p - 1, zz, piece],
+            psend.at[p - 1, zz, h], precv.at[p - 1, zz, h], xdev if p == 1 else ydev,
+        )
+
+    def zcopy(zz, up):
+        way = 1 if up else 0
+        to = at.device(z + 1 if up else z - 1, y, x, c)
+        return remote(mine.at[0, zz], z_in.at[way, zz], zsend.at[zz, way], zrecv.at[zz, way], to)
+
+    def add(into, terms, count):
+        def one(i, carry):
+            piece = pl.ds(pl.multiple_of(i * step, step), step)
+            total = into[piece].astype(jnp.float32)
+            for term in terms:
+                total = total + term[piece].astype(jnp.float32)
+            into[piece] = total.astype(into.dtype)
+            return carry
+
+        lax.fori_loop(0, count // step, one, 0)
+
+    def begin(off, zz):
+        for p in (3, 1, 2, 0):
+            load(p, zz).start()
+
+    def begin_cross(off, zz):
+        for p in (3, 1, 2, 0):
+            cross(p, zz).start()
+
+    def first(off, zz):
+        for p in (3, 1, 2, 0):
+            load(p, zz).wait()
+            cross(p, zz).wait_recv()
+            add(mine.at[p, zz], [theirs.at[p, zz]], rows)
+            if p == 3:
+                turn(1, zz).start()
+                turn(2, zz).start()
+            if p == 1:
+                plane(1, zz, 0).start()
+            if p == 2:
+                plane(2, zz, 1).start()
+
+    def second(off, zz):
+        turn(1, zz).wait_recv()
+        add(mine.at[2, zz, pl.ds(0, half)], [turned.at[0, zz]], half)
+        plane(2, zz, 0).start()
+        turn(2, zz).wait_recv()
+        add(mine.at[1, zz, pl.ds(half, half)], [turned.at[1, zz]], half)
+        plane(1, zz, 1).start()
+
+    def third(off, zz):
+        for p in (1, 2):
+            for h in (0, 1):
+                plane(p, zz, h).wait_recv()
+        add(mine.at[0, zz], [plane_in.at[0, zz], plane_in.at[1, zz]], rows)
+        if off <= 0:
+
+            @pl.when(z < depth - 1)
+            def _():
+                zcopy(zz, False).wait_recv()
+                add(mine.at[0, zz], [z_in.at[0, zz]], rows)
+
+        if off >= 0:
+
+            @pl.when(z > 0)
+            def _():
+                zcopy(zz, True).wait_recv()
+                add(mine.at[0, zz], [z_in.at[1, zz]], rows)
+
+        if off < 0:
+            zcopy(zz, False).start()
+        if off > 0:
+            zcopy(zz, True).start()
+        if off == 0:
+
+            def put(i, carry):
+                piece = pl.ds(pl.multiple_of(i * step, step), step)
+                out[piece] = mine[0, zz, piece]
+                return carry
+
+            lax.fori_loop(0, rows // step, put, 0)
+
+    def finish(off, zz):
+        for p in range(4):
+            cross(p, zz).wait_send()
+        for p in (1, 2):
+            turn(p, zz).wait_send()
+            plane(p, zz, 0).wait_send()
+            plane(p, zz, 1).wait_send()
+        if off < 0:
+            zcopy(zz, False).wait_send()
+        if off > 0:
+            zcopy(zz, True).wait_send()
+
+    for far in reversed(range(depth)):
+        at.at_distance(far, begin)
+    at.greet()
+    for far in reversed(range(depth)):
+        at.at_distance(far, begin_cross)
+    work = []
+    for far in range(depth):
+        turn_no = 2 * (depth - 1 - far)
+        work += [(turn_no, 0, first, far), (turn_no + 3, 1, second, far), (turn_no + 5, 2, third, far)]
+    for _, _, visit, far in sorted(work, key=lambda w: w[:2]):
+        at.at_distance(far, visit)
+    for far in range(depth):
+        at.at_distance(far, finish)
+
+
+def scatter_sums(sums, depth):
+    _, rows, width = sums.shape
+    sem = pltpu.SemaphoreType.DMA
+    vmem = lambda *lead: pltpu.VMEM(lead + (width,), sums.dtype)
+    return pl.pallas_call(
+        lambda *refs: scatter_kernel(depth, rows, *refs),
+        out_shape=jax.ShapeDtypeStruct((rows, width), sums.dtype),
+        in_specs=[pl.BlockSpec(memory_space=pl.ANY)],
+        out_specs=pl.BlockSpec(memory_space=pltpu.VMEM),
+        scratch_shapes=[
+            vmem(4, depth, rows), vmem(4, depth, rows), vmem(2, depth, rows // 2),
+            vmem(2, depth, rows), vmem(2, depth, rows),
+            sem((4, depth)), sem((4, depth)), sem((4, depth)), sem((2, depth)), sem((2, depth)),
+            sem((2, depth, 2)), sem((2, depth, 2)), sem((depth, 2)), sem((depth, 2)),
+        ],
+        compiler_params=pltpu.CompilerParams(
+            collective_id=1, has_side_effects=True, vmem_limit_bytes=48 * 1024 * 1024
+        ),
+        name="scatter_sums",
+    )(sums)
+
+
+def gathered_body(
+    tokens, norm_gain, router_weight, placement, expert_ids,
+    w_gate, w_up, w_down, shared_gate, shared_up, shared_down,
+):
+    node_count, local_count = lax.axis_size("node"), lax.axis_size("local")
+    peers = node_count * local_count
+    node, local = lax.axis_index("node"), lax.axis_index("local")
+    floats = tokens.astype(jnp.float32)
+    normed = (
+        floats * lax.rsqrt(jnp.mean(floats * floats, -1, keepdims=True) + 1e-06) * norm_gain
+    ).astype(jnp.bfloat16)
+    rows, width = normed.shape
+    experts, top_count = placement.shape[0], expert_ids.shape[1]
+    capacity = min(rows, 3 * rows * top_count // (2 * experts))
+    scores = jax.nn.sigmoid(jnp.dot(normed, router_weight, preferred_element_type=jnp.float32))
+    id_hot = expert_ids[:, :, None] == jnp.arange(experts, dtype=jnp.int32)
+    named = jnp.any(id_hot, 1)
+    chosen = jnp.where(named, scores, 0.0)
+    gates = chosen / jnp.sum(chosen, -1, keepdims=True)
+    lanes = -(-experts // 128) * 128
+    slot_hot = placement[:, None] == jnp.arange(lanes, dtype=jnp.int32)
+    by_slot = jnp.sum(jnp.where(slot_hot[None], gates[:, :, None], 0.0), 1).astype(jnp.bfloat16)
+    block = gather_rows(jnp.concatenate([normed, by_slot], 1), node_count // 2, peers)
+    all_rows = block[:, :, :width]
+    slot = (node * local_count + local) // 2
+    mine = jnp.arange(lanes, dtype=jnp.int32) == slot
+    weight = jnp.sum(jnp.where(mine, block[:, :, width:].astype(jnp.float32), 0.0), -1)
+    taken = weight > 0
+    spot = jnp.cumsum(taken.astype(jnp.int32), 1) - 1
+    row_hot = (spot[:, None, :] == jnp.arange(capacity, dtype=jnp.int32)[:, None]) & taken[:, None, :]
+    pick = row_hot.astype(jnp.bfloat16)
+    back = jnp.where(row_hot, weight[:, None, :], 0.0).astype(jnp.bfloat16)
+    packed = lax.dot_general(
+        pick, all_rows, (((2,), (1,)), ((0,), (0,))), preferred_element_type=jnp.float32
+    ).astype(jnp.bfloat16)
+    result = feed_forward(packed.reshape(peers * capacity, width), w_gate, w_up, w_down)
+    result = result.astype(jnp.bfloat16).reshape(peers, capacity, width)
+    sums = lax.dot_general(
+        back, result, (((1,), (1,)), ((0,), (0,))), preferred_element_type=jnp.float32
+    ).astype(jnp.bfloat16)
+    near = lax.dynamic_slice_in_dim(all_rows, node * local_count, local_count, 0)
+    shared = feed_forward(near.reshape(-1, width), shared_gate, shared_up, shared_down)
+    old = lax.dynamic_slice_in_dim(sums, node * local_count, local_count, 0)
+    new = (old.astype(jnp.float32) + shared.reshape(old.shape)).astype(jnp.bfloat16)
+    sums = lax.dynamic_update_slice_in_dim(sums, new, node * local_count, 0)
+    return scatter_sums(sums, node_count // 2)
+
+
 def solution(mesh):
     in_specs = (
         P(("node", "local"), None),
@@ -108,4 +486,14 @@
         P("local", None),
     )
     out_specs = P(("node", "local"), None)
-    return jax.shard_map(body, mesh=mesh, in_specs=in_specs, out_specs=out_specs, check_vma=False)
+    plane_of_four = mesh.shape["local"] == 4 and mesh.shape["node"] % 2 == 0
+
+    def chosen(*args):
+        pairs = mesh.size == 2 * args[3].shape[0]
+        small = args[0].size * args[0].dtype.itemsize <= 24 * 2**20
+        plan = gathered_body if plane_of_four and pairs and small else body
+        return jax.shard_map(
+            plan, mesh=mesh, in_specs=in_specs, out_specs=out_specs, check_vma=False
+        )(*args)
+
+    return chosen

time: 402 us -> 254 us (0.63)
  Pallas kernels: 0 us -> 163 us
  waiting for transfers between devices: 136 us -> 0 us
  blocking collectives: 124 us -> 0 us
  local copies, waits for them, and re-layouts: 48.8 us -> 9.23 us
  matrix products: 55.1 us -> 70.9 us
  between operations: 14 us -> 0.08 us
  other arithmetic: 15.9 us -> 10.9 us
  starting transfers between devices: 4.97 us -> 0 us
    pallas_call x0 -> x2, Pallas kernels: none -> 163 us  [the longest x1 81.6 us: gather_rows(): pl.pallas_call(lambda *refs: gather_kernel(depth, rows, *refs), out_shape...]
    all_to_all x1 -> x0, blocking collectives: 124 us -> none  [body(): lax.all_to_all(outgoing, ('node', 'local'), split_axis=0, concat_axis=0,...]
    all_to_all x1 -> x0, waiting for transfers between devices: 107 us -> none  [body(): lax.all_to_all(answers, ('node', 'local'), split_axis=0, concat_axis=0, t...]
    all_gather x1 -> x0, waiting for transfers between devices: 21.9 us -> none  [body(): gathered = lax.all_gather(normed, 'local', axis=0, tiled=True)]
    reshape x2 -> x0, local copies, waits for them, and re-layouts: 14.6 us -> none  [the longest x1 7.37 us: body(): expert_out = returned.reshape(experts * capacity, model_width)]
    dot_general x3, matrix products: 8.15 us -> 21.1 us  [the longest x1 10.7 us: gathered_body(): lax.dot_general(back, result, (((1,), (1,)), ((0,), (0,))), preferred_ele...]
    unnamed x25 -> x11, local copies, waits for them, and re-layouts: 11.4 us -> 3.13 us
    ppermute x2 -> x0, waiting for transfers between devices: 7.9 us -> none  [partner_2(): return lax.ppermute(block, axis, route)]
  transfers between devices with their start and end apart: 5 -> 0, of which waited for: 3 -> 0; matrix products, arithmetic and copies ran while one was open for 5% -> 0% of each run, Pallas kernels for 0% -> 0%
where the time goes in v1:
time: 254 us
  Pallas kernels  163 us (64%)
  matrix products  70.9 us (28%)
  other arithmetic  10.9 us (4%)
  local copies, waits for them, and re-layouts  9.23 us (4%)
    pallas_call x1, Pallas kernels, gather_rows(): pl.pallas_call(lambda *refs: gather_kernel(depth, rows, *refs), out_shape...  81.6 us
    pallas_call x1, Pallas kernels, scatter_sums(): pl.pallas_call(lambda *refs: scatter_kernel(depth, rows, *refs), out_shap...  80.9 us
    dot_general x2, matrix products, feed_forward(): return jnp.dot(activated, down_rows, preferred_element_type=jnp.float32)  34.1 us
    dot_general x2, matrix products, feed_forward(): jnp.dot(row_block, gate_cols, preferred_element_type=jnp.float32)  15.7 us
    dot_general x1, matrix products, gathered_body(): lax.dot_general(back, result, (((1,), (1,)), ((0,), (0,))), preferred_ele...  10.7 us
    dot_general x1, matrix products, gathered_body(): lax.dot_general(pick, all_rows, (((2,), (1,)), ((0,), (0,))), preferred_e...  9.32 us
    slice x2, local copies, waits for them, and re-layouts, gathered_body(): all_rows = block[:, :, :width]  5.77 us

profile of v1, /device:TPU:0, one launch (start us, length us, event | category | flops | bytes accessed | tf_op | source)
XLA Modules:
  0.0 253.6 jit_solution(15724797015061328323)
XLA Ops:
  0.0 0.0 copy-start
  0.0 1.4 fusion.9
  1.4 0.7 iota_compare_fusion.2
  2.1 0.7 fusion.19
  2.8 1.2 fusion.11
  4.1 1.1 fusion.25
  5.2 0.1 copy.14
  5.3 0.4 select_reduce_fusion.1
  5.7 0.8 pad_maximum_fusion.refs_0_
  6.5 81.6 %gather_rows.1 = bf16[32,128,2176]{2,1,0:T(8,128)(2,1)} custom-call(bf16[128,2176]{1,0:T(8,128)(2,1)} %pad_maximum_fusion.refs_0_), custom_call_target="tpu_custom_call" | custom-call | tf_op jit(solution)/shard_map/gather_rows/pallas_call | solution.py:248
  88.1 1.6 select_reduce_fusion
  89.8 0.3 reduce_window_sum.11
  90.1 9.3 %convolution_convert_fusion.2 = bf16[32,72,2048]{2,1,0:T(8,128)(2,1)} fusion(s32[32,128]{1,0:T(8,128)S(1)} %broadcast_add_fusion, pred[32,128]{1,0:T(8,128)(4,1)S(1)} %get-tuple-element.6, bf16[32,128,2176]{2,1,0:T(8,128)(2,1)} %gather_rows.1), kind=kOutput, calls=%fused_computation.3 | convolution fusion | flops 1213267968 | bytes 26234880 | tf_op jit(solution)/shard_map/dot_general | solution.py:458
  99.4 0.0 slice-start
  99.4 5.8 %slice-done = bf16[32,128,2048]{2,1,0:T(8,128)(2,1)S(1)} async-done(((bf16[32,128,2176]{2,1,0:T(8,128)(2,1)}), bf16[32,128,2048]{2,1,0:T(8,128)(2,1)S(1)}, s32[]{:S(2)}) %slice-start) | async-done | bytes 16777240 | tf_op jit(solution)/shard_map/slice | solution.py:449
  105.2 0.0 copy-start.4
  105.2 0.2 constant_dynamic-slice_fusion
  105.4 0.0 copy-start.3
  105.4 1.3 copy-done.3
  106.7 1.0 copy-done.4
  107.7 2.8 %fusion.27 = f32[512,704]{0,1:T(8,128)} fusion(bf16[512,2048]{1,0:T(8,128)(2,1)S(1)} %bitcast.21, bf16[2048,704]{0,1:T(8,128)(2,1)S(1)} %copy-done.4), kind=kOutput, calls=%fused_computation.48 | convolution fusion | flops 1476395008 | bytes 6422528 | tf_op jit(solution)/shard_map/dot_general | solution.py:20
  110.5 9.3 %fusion.12 = f32[512,2048]{1,0:T(8,128)} fusion(bf16[704,2048]{1,0:T(8,128)(2,1)} %param.21, bf16[512,2048]{1,0:T(8,128)(2,1)} %bitcast.22, bf16[2048,704]{0,1:T(8,128)(2,1)} %param.20, f32[512,704]{0,1:T(8,128)} %fusion.27), kind=kOutput, calls=%fused_computation.24 | convolution fusion | flops 2954952704 | bytes 13500416 | tf_op jit(solution)/shard_map/dot_general | solution.py:23
  119.8 12.9 %fusion.26 = f32[2304,704]{0,1:T(8,128)} fusion(bf16[2304,2048]{1,0:T(8,128)(2,1)} %bitcast.17, bf16[2048,704]{0,1:T(8,128)(2,1)} %param.16), kind=kOutput, calls=%fused_computation.47 | convolution fusion | flops 6643777536 | bytes 18808832 | tf_op jit(solution)/shard_map/dot_general | solution.py:20
  132.7 0.0 copy-done
  132.7 24.8 %convolution_convert_fusion.1 = bf16[2304,2048]{1,0:T(8,128)(2,1)} fusion(bf16[704,2048]{1,0:T(8,128)(2,1)S(1)} %copy-done, f32[2304,704]{0,1:T(8,128)} %fusion.26, bf16[2304,2048]{1,0:T(8,128)(2,1)} %bitcast.18, bf16[2048,704]{0,1:T(8,128)(2,1)} %param.17), kind=kOutput, calls=%fused_computation.1 | convolution fusion | flops 13302005760 | bytes 31129600 | tf_op jit(solution)/shard_map/dot_general | solution.py:23
  157.5 0.0 copy-start.2
  157.5 10.7 %convolution_convert_fusion = bf16[32,128,2048]{2,1,0:T(8,128)(2,1)} fusion(bf16[32,72,2048]{2,1,0:T(8,128)(2,1)} %bitcast.19, f32[32,128]{1,0:T(8,128)S(1)} %select_reduce_fusion, s32[32,128]{1,0:T(8,128)S(1)} %broadcast_add_fusion, pred[32,128]{1,0:T(8,128)(4,1)S(1)} %get-tuple-element.6), kind=kOutput, calls=%fused_computation | convolution fusion | flops 1217232896 | bytes 26251264 | tf_op jit(solution)/shard_map/dot_general | solution.py:463
  168.2 0.0 copy-done.2
  168.2 3.7 %fusion.1.refs_0_ = bf16[32,128,2048]{2,1,0:T(8,128)(2,1)} fusion(bf16[32,128,2048]{2,1,0:T(8,128)(2,1)} %convolution_convert_fusion, s32[]{:T(128)S(6)} %select_n.31, f32[4,128,2048]{2,1,0:T(8,128)S(1)} %bitcast.20), kind=kLoop, calls=%fused_computation.6 | loop fusion | flops 3145728 | bytes 8388612 | tf_op jit(solution)/shard_map/dynamic_update_slice | solution.py:470
  171.9 0.0 copy-start.1
  171.9 80.9 %scatter_sums.1 = bf16[128,2048]{1,0:T(8,128)(2,1)S(1)} custom-call(bf16[32,128,2048]{2,1,0:T(8,128)(2,1)} %fusion.1.refs_0_), custom_call_target="tpu_custom_call" | custom-call | tf_op jit(solution)/shard_map/scatter_sums/pallas_call | solution.py:408
  252.8 0.8 copy.17
  253.6 0.0 copy-done.1
  (5 shorter events, 0.0 us)
Async XLA Ops:
  0.0 132.7 %copy-start = (bf16[704,2048]{1,0:T(8,128)(2,1)S(1)}, bf16[704,2048]{1,0:T(8,128)(2,1)}, u32[]{:S(2)}) copy-start(bf16[704,2048]{1,0:T(8,128)(2,1)} %param.18) | copy-start | bytes 8650756
  99.4 5.8 %slice-start = ((bf16[32,128,2176]{2,1,0:T(8,128)(2,1)}), bf16[32,128,2048]{2,1,0:T(8,128)(2,1)S(1)}, s32[]{:S(2)}) async-start(bf16[32,128,2176]{2,1,0:T(8,128)(2,1)} %gather_rows.1), calls=%async_computation | async-start | bytes 33554432 | tf_op jit(solution)/shard_map/slice | solution.py:449
  105.2 2.6 %copy-start.4 = (bf16[2048,704]{0,1:T(8,128)(2,1)S(1)}, bf16[2048,704]{0,1:T(8,128)(2,1)}, u32[]{:S(2)}) copy-start(bf16[2048,704]{0,1:T(8,128)(2,1)} %param.19) | copy-start | bytes 8650756
  105.4 1.3 copy-start.3
  157.5 10.7 %copy-start.2 = (f32[512,2048]{1,0:T(8,128)S(1)}, f32[512,2048]{1,0:T(8,128)}, u32[]{:S(2)}) copy-start(f32[512,2048]{1,0:T(8,128)} %fusion.12) | copy-start | bytes 12582916
  171.9 81.7 %copy-start.1 = (bf16[704,2048]{1,0:T(8,128)(2,1)S(1)}, bf16[704,2048]{1,0:T(8,128)(2,1)}, u32[]{:S(2)}) copy-start(bf16[704,2048]{1,0:T(8,128)(2,1)} %param.18) | copy-start | bytes 8650756
